TPU v7x, 32 devices: a whole 2x2x4 slice. The times are simulated.
32 devices in a mesh: dp: 8 (over z, y), tensor: 4 (over x, core).
Axes of the slice: x: 2, y: 2, z: 4, core: 2. Of those that a mesh axis runs over, the one named last changes fastest.
Arguments:
- layer_input: bfloat16 [16384, 768], P(('dp', 'tensor')), may hold values from -6 to 6
- out_grad: bfloat16 [16384, 768], P(('dp', 'tensor')), may hold values from -6 to 6
- lengths: int32 [16], P('dp'), may hold values from 256 to 1024, as said below
- entry_weight: bfloat16 [768, 3, 768], P('dp', None, 'tensor'), may hold values from -0.21875 to 0.21875
- query_bias: float32 [768], replicated, may hold values from -3 to 3
- value_bias: float32 [768], replicated, may hold values from -3 to 3
- exit_weight: bfloat16 [768, 768], P('tensor', 'dp'), may hold values from -3.5 to 3.5
- exit_bias: float32 [768], replicated, may hold values from -2 to 2
- first_gain: float32 [768], replicated, may hold values from 0.5 to 1.5
- first_shift: float32 [768], replicated, may hold values from -1.5 to 1.5
- up_weight: bfloat16 [768, 3072], P('dp', 'tensor'), may hold values from -0.21875 to 0.21875
- up_bias: float32 [3072], replicated, may hold values from -3 to 3
- down_weight: bfloat16 [3072, 768], P('tensor', 'dp'), may hold values from -0.15625 to 0.15625
- down_bias: float32 [768], replicated, may hold values from -2 to 2
- second_gain: float32 [768], replicated, may hold values from 0.5 to 1.5
- second_shift: float32 [768], replicated, may hold values from -1.5 to 1.5
Outputs:
- layer_output: bfloat16 [16384, 768], P(('dp', 'tensor'))
- input_grad: float32 [16384, 768], P(('dp', 'tensor'))
- entry_grad: float32 [768, 3, 768], P('dp', None, 'tensor')
- query_bias_grad: float32 [768], replicated
- value_bias_grad: float32 [768], replicated
- exit_grad: float32 [768, 768], P('tensor', 'dp')
- exit_bias_grad: float32 [768], replicated
- first_gain_grad: float32 [768], replicated
- first_shift_grad: float32 [768], replicated
- up_grad: float32 [768, 3072], P('dp', 'tensor')
- up_bias_grad: float32 [3072], replicated
- down_grad: float32 [3072, 768], P('tensor', 'dp')
- down_bias_grad: float32 [768], replicated
- second_gain_grad: float32 [768], replicated
- second_shift_grad: float32 [768], replicated
Inputs may be any that keep to these rules, and one draw needn't show every extreme that they name: `lengths`: the number of leading tokens of each sequence that are not padding; some sequence is full and some has 256.
All inputs are finite; a program needn't handle non-finite values.
Results may differ from a plain program's by a relative error of at most 0.023.
Values may be sent and summed in bfloat16 or wider, within the bound.
A program may use at most 128 MiB of HBM per device.

v0:
```python
from functools import partial
import math
import jax
import jax.numpy as jnp
from jax import lax
from jax.sharding import PartitionSpec as P

HD = 64
LEN = 1024
EPSILON = 1e-12
NEG_FILL = -1e30


def layer_norm(rows, gain, shift):
    center = rows - jnp.mean(rows, axis=-1, keepdims=True)
    spread = jnp.mean(center * center, axis=-1, keepdims=True)
    return center * lax.rsqrt(spread + EPSILON) * gain + shift


def across(left, right):
    return lax.dot_general(
        left, right, (((0,), (0,)), ((), ())), preferred_element_type=jnp.float32
    )


def against(left, right):
    return lax.dot_general(
        left, right, (((1,), (1,)), ((), ())), preferred_element_type=jnp.float32
    )


def key_scores(queries, keys, length, scale):
    scores = jnp.einsum("qhd,khd->hqk", queries, keys, preferred_element_type=jnp.float32) * scale
    valid = jnp.arange(keys.shape[0]) < length
    return jnp.where(valid[None, None, :], scores, NEG_FILL)


def attend_sequence(item, scale, block):
    queries, keys, values, length = item
    blocks = queries.reshape(-1, block, queries.shape[1], queries.shape[2])

    def one_block(query_block):
        scores = key_scores(query_block, keys, length, scale)
        row_max = jnp.max(scores, axis=-1, keepdims=True)
        weights = jnp.exp(scores - row_max)
        total = jnp.sum(weights, axis=-1, keepdims=True)
        probs = (weights / total).astype(jnp.bfloat16)
        context = jnp.einsum("hqk,khd->qhd", probs, values, preferred_element_type=jnp.float32)
        return (context.astype(jnp.bfloat16), (row_max + jnp.log(total))[..., 0])

    return lax.map(one_block, blocks)


def attend_back(item, scale, block):
    queries, keys, values, length, context_grad, logsum = item
    heads = queries.shape[1]
    head_size = queries.shape[2]
    pieces = (
        queries.reshape(-1, block, heads, head_size),
        context_grad.reshape(-1, block, heads, head_size),
        logsum,
    )

    def one_block(carry, piece):
        key_total, value_total = carry
        query_block, grad_block, logsum_block = piece
        scores = key_scores(query_block, keys, length, scale)
        probs = jnp.exp(scores - logsum_block[..., None])
        value_total = value_total + jnp.einsum(
            "hqk,qhd->khd",
            probs.astype(jnp.bfloat16),
            grad_block,
            preferred_element_type=jnp.float32,
        )
        prob_grad = jnp.einsum(
            "qhd,khd->hqk", grad_block, values, preferred_element_type=jnp.float32
        )
        score_grad = (
            probs * (prob_grad - jnp.sum(probs * prob_grad, axis=-1, keepdims=True))
        ).astype(jnp.bfloat16)
        query_grad = (
            jnp.einsum("hqk,khd->qhd", score_grad, keys, preferred_element_type=jnp.float32) * scale
        )
        key_total = (
            key_total
            + jnp.einsum(
                "hqk,qhd->khd", score_grad, query_block, preferred_element_type=jnp.float32
            )
            * scale
        )
        return ((key_total, value_total), query_grad.astype(jnp.bfloat16))

    empty = jnp.zeros(keys.shape, jnp.float32)
    (key_total, value_total), query_grads = lax.scan(one_block, (empty, empty), pieces)
    return (
        query_grads.reshape(queries.shape),
        key_total.astype(jnp.bfloat16),
        value_total.astype(jnp.bfloat16),
    )


def place_slice(local, width, offset):
    return lax.dynamic_update_slice_in_dim(jnp.zeros((width,), jnp.float32), local, offset, 0)


def body(
    layer_input,
    out_grad,
    lengths,
    entry_weight,
    query_bias,
    value_bias,
    exit_weight,
    exit_bias,
    first_gain,
    first_shift,
    up_weight,
    up_bias,
    down_weight,
    down_bias,
    second_gain,
    second_shift,
):
    tensor_rank = lax.axis_index("tensor")
    own_rows = layer_input.shape[0]
    width = layer_input.shape[1]
    local_width = entry_weight.shape[2]
    local_hidden = up_weight.shape[1]
    full_hidden = up_bias.shape[0]
    head_count = local_width // HD
    seq_count = lengths.shape[0]
    group_rows = seq_count * LEN
    scale = 1.0 / math.sqrt(HD)
    block = min(512, LEN)
    entry_full, exit_full, up_full, down_full = (
        lax.all_gather(entry_weight, "dp", axis=0, tiled=True),
        lax.all_gather(exit_weight, "dp", axis=1, tiled=True),
        lax.all_gather(up_weight, "dp", axis=0, tiled=True),
        lax.all_gather(down_weight, "dp", axis=1, tiled=True),
    )
    entry_matrix = entry_full.reshape(width, 3 * local_width)
    query_local = lax.dynamic_slice_in_dim(query_bias, tensor_rank * local_width, local_width)
    value_local = lax.dynamic_slice_in_dim(value_bias, tensor_rank * local_width, local_width)
    up_local = lax.dynamic_slice_in_dim(up_bias, tensor_rank * local_hidden, local_hidden)
    rows_all = lax.all_gather(layer_input, "tensor", axis=0, tiled=True)
    offsets = jnp.stack([query_local, jnp.zeros_like(query_local), value_local])
    mixed = jnp.dot(rows_all, entry_matrix, preferred_element_type=jnp.float32).reshape(
        group_rows, 3, local_width
    )
    mixed = (mixed + offsets).astype(jnp.bfloat16)
    queries = mixed[:, 0].reshape(seq_count, LEN, head_count, HD)
    keys = mixed[:, 1].reshape(seq_count, LEN, head_count, HD)
    values = mixed[:, 2].reshape(seq_count, LEN, head_count, HD)
    context, logsum = lax.map(
        partial(attend_sequence, scale=scale, block=block), (queries, keys, values, lengths)
    )
    context = context.reshape(group_rows, local_width)
    attended = lax.psum_scatter(
        jnp.dot(context, exit_full, preferred_element_type=jnp.float32).astype(jnp.bfloat16),
        "tensor",
        scatter_dimension=0,
        tiled=True,
    ).astype(jnp.float32)
    first_sum = layer_input.astype(jnp.float32) + attended + exit_bias
    normed, first_pull = jax.vjp(layer_norm, first_sum, first_gain, first_shift)
    normed_low = normed.astype(jnp.bfloat16)
    normed_all = lax.all_gather(normed_low, "tensor", axis=0, tiled=True)
    upper = jnp.dot(normed_all, up_full, preferred_element_type=jnp.float32) + up_local
    active_full, gelu_pull = jax.vjp(partial(jax.nn.gelu, approximate=False), upper)
    active = active_full.astype(jnp.bfloat16)
    lowered = lax.psum_scatter(
        jnp.dot(
            lax.slice_in_dim(active, 0, lax.axis_size("tensor") * own_rows, axis=0),
            down_full,
            preferred_element_type=jnp.float32,
        ).astype(jnp.bfloat16),
        "tensor",
        scatter_dimension=0,
        tiled=True,
    ).astype(jnp.float32)
    second_sum = normed_low.astype(jnp.float32) + lowered + down_bias
    output, second_pull = jax.vjp(layer_norm, second_sum, second_gain, second_shift)
    layer_output = output.astype(jnp.bfloat16)
    entry_back, exit_back, up_back, down_back = (
        lax.all_gather(entry_weight, "dp", axis=0, tiled=True),
        lax.all_gather(exit_weight, "dp", axis=1, tiled=True),
        lax.all_gather(up_weight, "dp", axis=0, tiled=True),
        lax.all_gather(down_weight, "dp", axis=1, tiled=True),
    )
    entry_back_matrix = entry_back.reshape(width, 3 * local_width)
    second_grad, second_gain_grad, second_shift_grad = second_pull(out_grad.astype(jnp.float32))
    down_bias_grad = jnp.sum(second_grad, axis=0)
    lowered_all = lax.all_gather(second_grad.astype(jnp.bfloat16), "tensor", axis=0, tiled=True)
    down_grad_full = across(active, lowered_all)
    active_grad = against(lowered_all, down_back)
    upper_grad = gelu_pull(active_grad)[0].astype(jnp.bfloat16)
    up_bias_local = jnp.sum(upper_grad.astype(jnp.float32), axis=0)
    up_grad_full = across(normed_all, upper_grad)
    normed_back = lax.psum_scatter(
        against(upper_grad, up_back).astype(jnp.bfloat16), "tensor", scatter_dimension=0, tiled=True
    ).astype(jnp.float32)
    normed_grad = second_grad + normed_back
    first_grad, first_gain_grad, first_shift_grad = first_pull(normed_grad)
    exit_bias_grad = jnp.sum(first_grad, axis=0)
    attended_all = lax.all_gather(first_grad.astype(jnp.bfloat16), "tensor", axis=0, tiled=True)
    exit_grad_full = across(context, attended_all)
    context_grad = against(attended_all, exit_back).astype(jnp.bfloat16)
    query_grad, key_grad, value_grad = lax.map(
        partial(attend_back, scale=scale, block=block),
        (
            queries,
            keys,
            values,
            lengths,
            context_grad.reshape(seq_count, LEN, head_count, HD),
            logsum,
        ),
    )
    mixed_grad = jnp.stack(
        [
            query_grad.reshape(group_rows, local_width),
            key_grad.reshape(group_rows, local_width),
            value_grad.reshape(group_rows, local_width),
        ],
        axis=1,
    )
    query_bias_local = jnp.sum(mixed_grad[:, 0].astype(jnp.float32), axis=0)
    value_bias_local = jnp.sum(mixed_grad[:, 2].astype(jnp.float32), axis=0)
    mixed_flat = mixed_grad.reshape(group_rows, 3 * local_width)
    entry_grad_full = across(rows_all, mixed_flat).reshape(width, 3, local_width)
    input_back = lax.psum_scatter(
        against(mixed_flat, entry_back_matrix).astype(jnp.bfloat16),
        "tensor",
        scatter_dimension=0,
        tiled=True,
    ).astype(jnp.float32)
    input_grad = first_grad + input_back
    entry_grad, exit_grad, up_grad, down_grad = (
        lax.psum_scatter(entry_grad_full, "dp", scatter_dimension=0, tiled=True),
        lax.psum_scatter(exit_grad_full, "dp", scatter_dimension=1, tiled=True),
        lax.psum_scatter(up_grad_full, "dp", scatter_dimension=0, tiled=True),
        lax.psum_scatter(down_grad_full, "dp", scatter_dimension=1, tiled=True),
    )
    vectors = lax.psum(
        (
            place_slice(query_bias_local, width, tensor_rank * local_width),
            place_slice(value_bias_local, width, tensor_rank * local_width),
            exit_bias_grad,
            first_gain_grad,
            first_shift_grad,
            place_slice(up_bias_local, full_hidden, tensor_rank * local_hidden),
            down_bias_grad,
            second_gain_grad,
            second_shift_grad,
        ),
        ("dp", "tensor"),
    )
    return (
        layer_output,
        input_grad,
        entry_grad,
        vectors[0],
        vectors[1],
        exit_grad,
        vectors[2],
        vectors[3],
        vectors[4],
        up_grad,
        vectors[5],
        down_grad,
        vectors[6],
        vectors[7],
        vectors[8],
    )


def solution(mesh):
    return jax.shard_map(
        body,
        mesh=mesh,
        in_specs=(
            P(("dp", "tensor"), None),
            P(("dp", "tensor"), None),
            P("dp"),
            P("dp", None, "tensor"),
            P(),
            P(),
            P("tensor", "dp"),
            P(),
            P(),
            P(),
            P("dp", "tensor"),
            P(),
            P("tensor", "dp"),
            P(),
            P(),
            P(),
        ),
        out_specs=(
            P(("dp", "tensor"), None),
            P(("dp", "tensor"), None),
            P("dp", None, "tensor"),
            P(),
            P(),
            P("tensor", "dp"),
            P(),
            P(),
            P(),
            P("dp", "tensor"),
            P(),
            P("tensor", "dp"),
            P(),
            P(),
            P(),
        ),
        check_vma=False,
    )
```

profile of v0, /device:TPU:0, one launch (start us, length us, event | category | flops | bytes accessed | tf_op | source)
XLA Modules:
  0.0 812.9 jit_solution(9412491876366717269)
XLA Ops:
  11.2 35.4 %all_gather.29 = bf16[768,3,192]{2,0,1:T(8,128)(2,1)S(1)} all-gather(bf16[96,3,192]{2,0,1:T(8,128)(2,1)} %param.27), channel_id=1, replica_groups=mesh['dp'=8,'tensor'=4] {'dp'}, dimensions={0}, use_global_device_ids=true | all-gather | bytes 995328 | tf_op jit(solution)/shard_map/all_gather | solution.py:136
  47.4 33.0 %all_gather.30 = bf16[192,768]{0,1:T(8,128)(2,1)} all-gather(bf16[192,96]{0,1:T(8,128)(2,1)S(1)} %copy.73), channel_id=1, replica_groups=mesh['dp'=8,'tensor'=4] {'dp'}, dimensions={1}, use_global_device_ids=true | all-gather | bytes 331776 | tf_op jit(solution)/shard_map/all_gather | solution.py:137
  88.7 32.5 %while.54 = (s32[]{:T(128)}, bf16[2,2,512,3,64]{2,1,0,4,3:T(2,128)(2,1)}, f32[2,2,3,512]{3,2,1,0:T(4,128)}, bf16[2,1024,3,64]{1,3,2,0:T(8,128)(2,1)}, bf16[2,102...) while((s32[]{:T(128)}, ...), condition=%wide.region_5.6_spmd, body=%wide.region_0.5_spmd.sunk | while | flops 421625344 | bytes 24865084 | solution.py:154
  92.4 10.8 %while.57 = (s32[]{:T(128)}, bf16[2,512,3,64]{1,3,2,0:T(8,128)(2,1)S(1)}, f32[2,3,512]{2,1,0:T(4,128)S(1)}, s32[]{:T(128)}, bf16[2,512,3,64]{1,3,2,0:T(8,128)(2,...) while((s32[]{:T(128)}, bf16[2,512,3,64]{1,3,2,0:T(8,128)(2,1)S(1)}, ...), condition=%wide.region_4.4_spmd, body=%wide.region_1.3_spmd.sunk | while | flops 421625344 | bytes 20117612 | solution.py:51
  108.6 10.8 %while.57 = (s32[]{:T(128)}, bf16[2,512,3,64]{1,3,2,0:T(8,128)(2,1)S(1)}, f32[2,3,512]{2,1,0:T(4,128)S(1)}, s32[]{:T(128)}, bf16[2,512,3,64]{1,3,2,0:T(8,128)(2,...) while((s32[]{:T(128)}, bf16[2,512,3,64]{1,3,2,0:T(8,128)(2,1)S(1)}, ...), condition=%wide.region_4.4_spmd, body=%wide.region_1.3_spmd.sunk | while | flops 421625344 | bytes 20117612 | solution.py:51
  127.4 37.9 %reduce-scatter.11.cloned.1.call-done = bf16[512,768]{1,0:T(8,128)(2,1)} async-done(((bf16[2048,768]{1,0:T(8,128)(2,1)}), bf16[512,768]{1,0:T(8,128)(2,1)}) %reduce-scatter.11.cloned.1.call-update) | async-done | bytes 786448 | tf_op jit(solution)/shard_map/reduce_scatter | solution.py:158
  171.4 28.8 %all-gather.9.cloned.1.call-done = bf16[2048,768]{1,0:T(8,128)(2,1)} async-done(((bf16[512,768]{1,0:T(8,128)(2,1)}), bf16[2048,768]{1,0:T(8,128)(2,1)}) %all-gather.9.cloned.1.call-update) | async-done | bytes 3145744 | tf_op jit(solution)/shard_map/all_gather | solution.py:167
  200.2 19.0 %multiply_convert_fusion.1 = (bf16[2048,768]{1,0:T(8,128)(2,1)}, f32[2048,768]{1,0:T(8,128)}, f32[2048,768]{1,0:T(8,128)}) fusion(f32[768]{0:T(1024)S(1)} %dynamic_slice.58, bf16[2048,768]{1,0:T(8,128)(2,1)} %all-gather.9.cloned.1.call-done, bf16[768,768]{1,0:T(8,128)(2,1)} %all-gather.11.cloned.1.call-done), kind=kOutput, calls=%fused_computation.68 | convolution fusion | flops 2519728128 | bytes 20057088 | tf_op jit(solution)/shard_map/dot_general | solution.py:168
  219.1 24.5 %all-gather.13.cloned.1.call-done = bf16[768,768]{0,1:T(8,128)(2,1)} async-done(((bf16[768,96]{0,1:T(8,128)(2,1)}), bf16[768,768]{0,1:T(8,128)(2,1)}) %all-gather.13.cloned.1.call-update) | async-done | bytes 1179664 | tf_op jit(solution)/shard_map/all_gather | solution.py:139
  250.3 36.1 %reduce-scatter.13.cloned.1.call-done = bf16[512,768]{1,0:T(8,128)(2,1)} async-done(((bf16[2048,768]{1,0:T(8,128)(2,1)}), bf16[512,768]{1,0:T(8,128)(2,1)}) %reduce-scatter.13.cloned.1.call-update) | async-done | bytes 786448 | tf_op jit(solution)/shard_map/reduce_scatter | solution.py:171
  295.4 28.2 %all-gather.15.cloned.1.call-done = bf16[2048,768]{1,0:T(8,128)(2,1)} async-done(((bf16[512,768]{1,0:T(8,128)(2,1)}), bf16[2048,768]{1,0:T(8,128)(2,1)}) %all-gather.15.cloned.1.call-update) | async-done | bytes 3145744 | tf_op jit(solution)/shard_map/all_gather | solution.py:193
  323.6 11.1 %convert_reduce_fusion = (f32[768]{0:T(1024)}, bf16[2048,768]{1,0:T(8,128)(2,1)S(1)}) fusion(f32[2048,768]{1,0:T(8,128)} %get-tuple-element.413, f32[2048,768]{1,0:T(8,128)} %get-tuple-element.428, f32[768]{0:T(1024)S(1)} %copy-done.40, bf16[2048,768]{1,0:T(8,128)(2,1)} %all-gather.15.cloned.1.call-done, bf16[768,768]{0,1:T(8,128)(2,1)} %all-gather.13.cloned.1.call-done), kind=kOutput, calls=%fused_computation.66 | convolution fusion | flops 2442657024 | bytes 20060160 | tf_op jit(solution)/shard_map/dot_general | solution.py:27
  340.6 37.8 %reduce-scatter.15.cloned.1.call-done = bf16[512,768]{1,0:T(8,128)(2,1)} async-done(((bf16[2048,768]{1,0:T(8,128)(2,1)}), bf16[512,768]{1,0:T(8,128)(2,1)}) %reduce-scatter.15.cloned.1.call-update) | async-done | bytes 786448 | tf_op jit(solution)/shard_map/reduce_scatter | solution.py:199
  387.0 28.4 %all-gather.17.cloned.1.call-done = bf16[2048,768]{1,0:T(8,128)(2,1)} async-done(((bf16[512,768]{1,0:T(8,128)(2,1)}), bf16[2048,768]{1,0:T(8,128)(2,1)}) %all-gather.17.cloned.1.call-update) | async-done | bytes 3145744 | tf_op jit(solution)/shard_map/all_gather | solution.py:205
  420.2 57.5 %while.56 = (s32[]{:T(128)}, bf16[2,1024,3,64]{3,2,1,0:T(4,128)(2,1)}, bf16[2,1024,3,64]{1,3,2,0:T(8,128)(2,1)}, bf16[2,1024,3,64]{1,3,2,0:T(8,128)(2,1)}, bf16[...) while((s32[]{:T(128)}, ...), condition=%wide.region_21.22_spmd, body=%wide.region_17.21_spmd.sunk | while | flops 1031798272 | bytes 74459688 | solution.py:208
  426.0 18.2 %while.58 = (s32[]{:T(128)}, f32[1024,3,64]{0,2,1:T(8,128)S(1)}, f32[1024,3,64]{0,2,1:T(8,128)}, bf16[2,512,3,64]{1,3,2,0:T(8,128)(2,1)S(1)}, bf16[2,512,3,64]{1...) while((s32[]{:T(128)}, f32[1024,3,64]{0,2,1:T(8,128)S(1)}, ...), condition=%wide.region_20.20_spmd.clone, body=%wide.region_18.19_spmd.clone.sunk | while | flops 1031405056 | bytes 58837208 | solution.py:94
  454.7 18.2 %while.58 = (s32[]{:T(128)}, f32[1024,3,64]{0,2,1:T(8,128)S(1)}, f32[1024,3,64]{0,2,1:T(8,128)}, bf16[2,512,3,64]{1,3,2,0:T(8,128)(2,1)S(1)}, bf16[2,512,3,64]{1...) while((s32[]{:T(128)}, f32[1024,3,64]{0,2,1:T(8,128)S(1)}, ...), condition=%wide.region_20.20_spmd.clone, body=%wide.region_18.19_spmd.clone.sunk | while | flops 1031405056 | bytes 58837208 | solution.py:94
  504.5 7.0 fusion.70
  511.9 7.0 fusion.71
  530.5 40.9 %all-reduce = (f32[768]{0:T(1024)}, f32[768]{0:T(1024)}, f32[768]{0:T(1024)}, f32[768]{0:T(1024)}, f32[768]{0:T(1024)}, /*index=5*/f32[3072]{0:T(1024)}, f32[768]{0:T(1024)}, f32[768]{0:T(1024)}, f32[768]{0:T(1024)}) all-reduce(f32[768]{0:T(1024)S(1)} %dynamic_update_slice.38, ...), channel_id=1, replica_groups=mesh['dp'=8,'tensor'=4] {'dp','tensor'}, use_global_device_ids=true, to_apply=%region_25.26 | all-reduce | flops 9216 | bytes 73728 | tf_op jit(solution)/shard_map/psum | solution.py:244
  573.0 12.3 %reduce-scatter.17.cloned.1.call-done = bf16[512,768]{1,0:T(8,128)(2,1)} async-done(((bf16[2048,768]{1,0:T(8,128)(2,1)}), bf16[512,768]{1,0:T(8,128)(2,1)}) %reduce-scatter.17.cloned.1.call-update) | async-done | bytes 786448 | tf_op jit(solution)/shard_map/reduce_scatter | solution.py:231
  587.8 71.2 %reduce-scatter.21.cloned.1.call-done = f32[96,768]{1,0:T(8,128)} async-done(((f32[768,768]{1,0:T(8,128)}), f32[96,768]{1,0:T(8,128)}) %reduce-scatter.21.cloned.1.call-update) | async-done | bytes 294928 | tf_op jit(solution)/shard_map/reduce_scatter | solution.py:241
  659.1 72.9 %reduce-scatter.23.cloned.1.call-done = f32[768,96]{0,1:T(8,128)} async-done(((f32[768,768]{0,1:T(8,128)}), f32[768,96]{0,1:T(8,128)}) %reduce-scatter.23.cloned.1.call-update) | async-done | bytes 294928 | tf_op jit(solution)/shard_map/reduce_scatter | solution.py:242
  732.0 73.3 %reduce-scatter.19.cloned.1.call-done = f32[96,3,192]{2,0,1:T(8,128)} async-done(((f32[768,3,192]{2,0,1:T(8,128)}), f32[96,3,192]{2,0,1:T(8,128)}) %reduce-scatter.19.cloned.1.call-update) | async-done | bytes 221200 | tf_op jit(solution)/shard_map/reduce_scatter | solution.py:239
  (308 shorter events, 191.0 us)
Async XLA Ops:
  8.0 72.4 %all-gather.7.cloned.1.call-start = ((), (), s32[]{:S(2)}) async-start(), calls=%async_computation.8 | async-start | bytes 3932160 | tf_op jit(solution)/shard_map/all_gather | solution.py:145
  8.7 156.6 %reduce-scatter.11.cloned.1.call-start = ((), (), s32[]{:S(2)}) async-start(), calls=%async_computation.9 | async-start | bytes 3932160 | tf_op jit(solution)/shard_map/reduce_scatter | solution.py:158
  123.7 41.6 %copy-start = (bf16[512,768]{1,0:T(8,128)(2,1)S(1)}, bf16[512,768]{1,0:T(8,128)(2,1)}, u32[]{:S(2)}) copy-start(bf16[512,768]{1,0:T(8,128)(2,1)} %param.24) | copy-start | bytes 2359300
  123.8 41.6 %copy-start.21 = (f32[768]{0:T(1024)S(1)}, f32[768]{0:T(1024)}, u32[]{:S(2)}) copy-start(f32[768]{0:T(1024)} %param.31) | copy-start | bytes 9220
  126.5 42.0 %copy-start.23 = (f32[768]{0:T(1024)S(1)}, f32[768]{0:T(1024)}, u32[]{:S(2)}) copy-start(f32[768]{0:T(1024)} %param.32) | copy-start | bytes 9220
  126.5 42.0 %copy-start.37 = (f32[768]{0:T(1024)S(1)}, f32[768]{0:T(1024)}, u32[]{:S(2)}) copy-start(f32[768]{0:T(1024)} %param.33) | copy-start | bytes 9220
  126.5 44.9 %all-gather.11.cloned.1.call-start = ((), (), s32[]{:S(2)}) async-start(), calls=%async_computation.11 | async-start | bytes 1327104 | tf_op jit(solution)/shard_map/all_gather | solution.py:138
  127.1 73.1 %all-gather.9.cloned.1.call-start = ((), (), s32[]{:S(2)}) async-start(), calls=%async_computation.10 | async-start | bytes 3932160 | tf_op jit(solution)/shard_map/all_gather | solution.py:167
  168.4 50.7 %copy-start.29 = (f32[512]{0:T(512)}, f32[512]{0:T(512)S(1)}, u32[]{:S(2)}) copy-start(f32[512]{0:T(512)S(1)} %multiply_reduce_fusion.4) | copy-start | bytes 6148
  168.5 50.6 %copy-start.24 = (f32[512]{0:T(512)}, f32[512]{0:T(512)S(1)}, u32[]{:S(2)}) copy-start(f32[512]{0:T(512)S(1)} %fusion.62) | copy-start | bytes 6148
  169.9 73.8 %all-gather.13.cloned.1.call-start = ((), (), s32[]{:S(2)}) async-start(), calls=%async_computation.12 | async-start | bytes 1327104 | tf_op jit(solution)/shard_map/all_gather | solution.py:139
  170.5 116.0 %reduce-scatter.13.cloned.1.call-start = ((), (), s32[]{:S(2)}) async-start(), calls=%async_computation.13 | async-start | bytes 3932160 | tf_op jit(solution)/shard_map/reduce_scatter | solution.py:171
  171.3 47.8 %copy-start.39 = (f32[768]{0:T(1024)}, f32[768]{0:T(1024)S(1)}, u32[]{:S(2)}) copy-start(f32[768]{0:T(1024)S(1)} %dynamic_slice.58) | copy-start | bytes 9220
  250.2 73.4 %all-gather.15.cloned.1.call-start = ((), (), s32[]{:S(2)}) async-start(), calls=%async_computation.14 | async-start | bytes 3932160 | tf_op jit(solution)/shard_map/all_gather | solution.py:193
  292.8 42.0 %copy-start.26 = (f32[512]{0:T(512)}, f32[512]{0:T(512)S(1)}, u32[]{:S(2)}) copy-start(f32[512]{0:T(512)S(1)} %negate_multiply_fusion.2) | copy-start | bytes 6148
  295.0 83.4 %reduce-scatter.15.cloned.1.call-start = ((), (), s32[]{:S(2)}) async-start(), calls=%async_computation.15 | async-start | bytes 3932160 | tf_op jit(solution)/shard_map/reduce_scatter | solution.py:199
  340.5 74.9 %all-gather.17.cloned.1.call-start = ((), (), s32[]{:S(2)}) async-start(), calls=%async_computation.16 | async-start | bytes 3932160 | tf_op jit(solution)/shard_map/all_gather | solution.py:205
  386.8 184.6 %reduce-scatter.25.cloned.1.call-start = ((), (), s32[]{:S(2)}) async-start(), calls=%async_computation.21 | async-start | bytes 884736
  482.2 103.1 %reduce-scatter.17.cloned.1.call-start = ((), (), s32[]{:S(2)}) async-start(), calls=%async_computation.17 | async-start | bytes 3932160 | tf_op jit(solution)/shard_map/reduce_scatter | solution.py:231
  504.5 154.6 %reduce-scatter.21.cloned.1.call-start = ((), (), s32[]{:S(2)}) async-start(), calls=%async_computation.19 | async-start | bytes 2654208 | tf_op jit(solution)/shard_map/reduce_scatter | solution.py:241
  511.6 220.4 %reduce-scatter.23.cloned.1.call-start = ((), (), s32[]{:S(2)}) async-start(), calls=%async_computation.20 | async-start | bytes 2654208 | tf_op jit(solution)/shard_map/reduce_scatter | solution.py:242
  518.9 286.4 %reduce-scatter.19.cloned.1.call-start = ((), (), s32[]{:S(2)}) async-start(), calls=%async_computation.18 | async-start | bytes 2654208 | tf_op jit(solution)/shard_map/reduce_scatter | solution.py:239
  525.5 59.8 %copy-start.10 = (f32[512,768]{1,0:T(8,128)S(1)}, f32[512,768]{1,0:T(8,128)}, u32[]{:S(2)}) copy-start(f32[512,768]{1,0:T(8,128)} %copy-done.9) | copy-start | bytes 4718596
  525.6 59.8 %copy-start.28 = (f32[512]{0:T(512)S(1)}, f32[512]{0:T(512)}, u32[]{:S(2)}) copy-start(f32[512]{0:T(512)} %copy-done.27) | copy-start | bytes 6148
  (42 other events, 406.0 us)
Sparse Core Ops, SparseCore 0:
  10.4 31.2 all-gather.6
  126.6 38.6 reduce-scatter.10
  295.1 28.5 all-gather.14
  386.9 28.4 all-gather.16
Sparse Core Ops, SparseCore 1:
  129.2 42.1 all-gather.10
  173.4 26.7 all-gather.8
  202.2 41.4 all-gather.12
  250.3 36.1 reduce-scatter.12
  340.6 37.7 reduce-scatter.14
  482.3 63.3 reduce-scatter.24
  548.0 37.2 reduce-scatter.16
  589.3 69.7 reduce-scatter.20
  663.0 68.9 reduce-scatter.22
  736.1 69.2 reduce-scatter.18
where the time goes:
time: 823 us; the launch traced here: 813 us
  waiting for transfers between devices  454 us (55%)
  matrix products  118 us (14%)
  blocking collectives  109 us (13%)
  local copies, waits for them, and re-layouts  66.9 us (8%)
  other arithmetic  46.2 us (6%)
  between operations  16.3 us (2%)
    reduce_scatter x1, waiting for transfers between devices, body(): lax.psum_scatter(entry_grad_full, 'dp', scatter_dimension=0, tiled=True)  73.3 us
    reduce_scatter x1, waiting for transfers between devices, body(): lax.psum_scatter(down_grad_full, 'dp', scatter_dimension=1, tiled=True)  72.9 us
    reduce_scatter x1, waiting for transfers between devices, body(): lax.psum_scatter(up_grad_full, 'dp', scatter_dimension=0, tiled=True)  71.2 us
    psum x1, blocking collectives, body(): lax.psum((place_slice(query_bias_local, width, tensor_rank * local_width)...  40.9 us
    reduce_scatter x1, waiting for transfers between devices, body(): lax.psum_scatter(jnp.dot(context, exit_full, preferred_element_type=jnp.f...  37.9 us
    reduce_scatter x1, waiting for transfers between devices, body(): lax.psum_scatter(against(upper_grad, up_back).astype(jnp.bfloat16), 'tens...  37.8 us
    reduce_scatter x1, waiting for transfers between devices, body(): lax.psum_scatter(jnp.dot(lax.slice_in_dim(active, 0, lax.axis_size('tenso...  36.1 us
    all_gather x1, blocking collectives, body(): lax.all_gather(entry_weight, 'dp', axis=0, tiled=True)  35.4 us
  transfers between devices with their start and end apart: 14, of which 12 were waited for; matrix products, arithmetic and copies ran while one was open for 10% of the time, Pallas kernels for 0%

commit v1 on v0

--- a/solution.py
+++ b/solution.py
@@ -1,14 +1,38 @@
+import functools
 from functools import partial
 import math
 import jax
 import jax.numpy as jnp
 from jax import lax
 from jax.sharding import PartitionSpec as P
+from jax.lax import axis_index, axis_size, ppermute
 
 HD = 64
 LEN = 1024
 EPSILON = 1e-12
 NEG_FILL = -1e30
+
+
+def register_members_all(inputs, along_axis):
+    ready = axis_size(along_axis)
+    aux, new, low = (ready, axis_index(along_axis), inputs.shape[1])
+    spare, odd = (inputs, 1)
+    while odd < aux:
+        spare = jnp.concatenate(
+            [
+                spare,
+                ppermute(
+                    spare, along_axis, perm=list(map(lambda s: (s, (s - odd) % aux), range(aux)))
+                ),
+            ],
+            axis=1,
+        )
+        odd = 2 * odd
+    passed = jnp.roll(spare, shift=new * low, axis=1)
+    return passed
+
+
+list_spots = functools.partial(register_members_all, along_axis="dp")
 
 
 def layer_norm(rows, gain, shift):
@@ -136,7 +160,7 @@
         lax.all_gather(entry_weight, "dp", axis=0, tiled=True),
         lax.all_gather(exit_weight, "dp", axis=1, tiled=True),
         lax.all_gather(up_weight, "dp", axis=0, tiled=True),
-        lax.all_gather(down_weight, "dp", axis=1, tiled=True),
+        list_spots(down_weight),
     )
     entry_matrix = entry_full.reshape(width, 3 * local_width)
     query_local = lax.dynamic_slice_in_dim(query_bias, tensor_rank * local_width, local_width)

time: 823 us -> 853 us (1.036)
  waiting for transfers between devices: 454 us -> 470 us
    ppermute x0 -> x3, waiting for transfers between devices: none -> 32.6 us  [register_members_all(): ppermute(spare, along_axis, perm=list(map(lambda s: (s, (s - odd) % aux),...]
    all_gather x1, waiting for transfers between devices: 28.8 us -> 0.01 us  [body(): normed_all = lax.all_gather(normed_low, 'tensor', axis=0, tiled=True)]
    all_gather x1, waiting for transfers between devices: 24.5 us -> 34.7 us  [body(): lax.all_gather(down_weight, 'dp', axis=1, tiled=True)]
  transfers between devices with their start and end apart: 14 -> 17, of which waited for: 12 -> 13; matrix products, arithmetic and copies ran while one was open for 10% -> 9% of each run, Pallas kernels for 0% -> 0%
where the time goes in v1:
time: 853 us; the launch traced here: 843 us
  waiting for transfers between devices  470 us (55%)
  matrix products  117 us (14%)
  blocking collectives  109 us (13%)
  local copies, waits for them, and re-layouts  74.6 us (9%)
  other arithmetic  47.1 us (6%)
  between operations  16.3 us (2%)
    reduce_scatter x1, waiting for transfers between devices, body(): lax.psum_scatter(down_grad_full, 'dp', scatter_dimension=1, tiled=True)  73.2 us
    reduce_scatter x1, waiting for transfers between devices, body(): lax.psum_scatter(entry_grad_full, 'dp', scatter_dimension=0, tiled=True)  73.1 us
    reduce_scatter x1, waiting for transfers between devices, body(): lax.psum_scatter(up_grad_full, 'dp', scatter_dimension=0, tiled=True)  71.2 us
    psum x1, blocking collectives, body(): lax.psum((place_slice(query_bias_local, width, tensor_rank * local_width)...  40.9 us
    reduce_scatter x1, waiting for transfers between devices, body(): lax.psum_scatter(against(upper_grad, up_back).astype(jnp.bfloat16), 'tens...  38 us
    reduce_scatter x1, waiting for transfers between devices, body(): lax.psum_scatter(jnp.dot(lax.slice_in_dim(active, 0, lax.axis_size('tenso...  38 us
    reduce_scatter x1, waiting for transfers between devices, body(): lax.psum_scatter(jnp.dot(context, exit_full, preferred_element_type=jnp.f...  38 us
    all_gather x1, blocking collectives, body(): lax.all_gather(entry_weight, 'dp', axis=0, tiled=True)  35.4 us
  transfers between devices with their start and end apart: 17, of which 13 were waited for; matrix products, arithmetic and copies ran while one was open for 9% of the time, Pallas kernels for 0%

profile of v1, /device:TPU:0, one launch (start us, length us, event | category | flops | bytes accessed | tf_op | source)
XLA Modules:
  0.0 842.8 jit_solution(3630657457750057699)
XLA Ops:
  11.2 35.4 %all_gather.28 = bf16[768,3,192]{2,0,1:T(8,128)(2,1)S(1)} all-gather(bf16[96,3,192]{2,0,1:T(8,128)(2,1)} %param.27), channel_id=1, replica_groups=mesh['dp'=8,'tensor'=4] {'dp'}, dimensions={0}, use_global_device_ids=true | all-gather | bytes 995328 | tf_op jit(solution)/shard_map/all_gather | solution.py:160
  47.4 33.0 %all_gather.29 = bf16[192,768]{0,1:T(8,128)(2,1)} all-gather(bf16[192,96]{0,1:T(8,128)(2,1)S(1)} %copy.73), channel_id=1, replica_groups=mesh['dp'=8,'tensor'=4] {'dp'}, dimensions={1}, use_global_device_ids=true | all-gather | bytes 331776 | tf_op jit(solution)/shard_map/all_gather | solution.py:161
  88.7 32.5 %while.54 = (s32[]{:T(128)}, bf16[2,2,512,3,64]{2,1,0,4,3:T(2,128)(2,1)}, f32[2,2,3,512]{3,2,1,0:T(4,128)}, bf16[2,1024,3,64]{1,3,2,0:T(8,128)(2,1)}, bf16[2,102...) while((s32[]{:T(128)}, ...), condition=%wide.region_5.6_spmd, body=%wide.region_0.5_spmd.sunk | while | flops 421625344 | bytes 24865084 | solution.py:178
  92.4 10.8 %while.57 = (s32[]{:T(128)}, bf16[2,512,3,64]{1,3,2,0:T(8,128)(2,1)S(1)}, f32[2,3,512]{2,1,0:T(4,128)S(1)}, s32[]{:T(128)}, bf16[2,512,3,64]{1,3,2,0:T(8,128)(2,...) while((s32[]{:T(128)}, bf16[2,512,3,64]{1,3,2,0:T(8,128)(2,1)S(1)}, ...), condition=%wide.region_4.4_spmd, body=%wide.region_1.3_spmd.sunk | while | flops 421625344 | bytes 20117612 | solution.py:75
  108.6 10.8 %while.57 = (s32[]{:T(128)}, bf16[2,512,3,64]{1,3,2,0:T(8,128)(2,1)S(1)}, f32[2,3,512]{2,1,0:T(4,128)S(1)}, s32[]{:T(128)}, bf16[2,512,3,64]{1,3,2,0:T(8,128)(2,...) while((s32[]{:T(128)}, bf16[2,512,3,64]{1,3,2,0:T(8,128)(2,1)S(1)}, ...), condition=%wide.region_4.4_spmd, body=%wide.region_1.3_spmd.sunk | while | flops 421625344 | bytes 20117612 | solution.py:75
  127.4 38.0 %reduce-scatter.11.cloned.1.call-done = bf16[512,768]{1,0:T(8,128)(2,1)} async-done(((bf16[2048,768]{1,0:T(8,128)(2,1)}), bf16[512,768]{1,0:T(8,128)(2,1)}) %reduce-scatter.11.cloned.1.call-update) | async-done | bytes 786448 | tf_op jit(solution)/shard_map/reduce_scatter | solution.py:182
  189.4 23.5 %collective-permute-done.2 = bf16[768,384]{0,1:T(8,128)(2,1)S(1)} collective-permute-done((bf16[768,384]{0,1:T(8,128)(2,1)}, bf16[768,384]{0,1:T(8,128)(2,1)S(1)}, u32[]{:S(2)}, u32[]{:S(2)}) %collective-permute-start.2) | collective-permute-done | bytes 589856 | tf_op jit(solution)/shard_map/ppermute | solution.py:24
  216.7 18.7 %multiply_convert_fusion.1 = (bf16[2048,768]{1,0:T(8,128)(2,1)S(1)}, f32[2048,768]{1,0:T(8,128)}, f32[2048,768]{1,0:T(8,128)}) fusion(f32[768]{0:T(1024)S(1)} %dynamic_slice.62, bf16[2048,768]{1,0:T(8,128)(2,1)} %all-gather.9.cloned.1.call-done, bf16[768,768]{1,0:T(8,128)(2,1)} %all-gather.11.cloned.1.call-done), kind=kOutput, calls=%fused_computation.68 | convolution fusion | flops 2519728128 | bytes 20057088 | tf_op jit(solution)/shard_map/dot_general | solution.py:192
  243.3 38.0 %reduce-scatter.13.cloned.1.call-done = bf16[512,768]{1,0:T(8,128)(2,1)} async-done(((bf16[2048,768]{1,0:T(8,128)(2,1)}), bf16[512,768]{1,0:T(8,128)(2,1)}) %reduce-scatter.13.cloned.1.call-update) | async-done | bytes 786448 | tf_op jit(solution)/shard_map/reduce_scatter | solution.py:195
  290.3 34.7 %all-gather.15.cloned.1.call-done = bf16[768,768]{0,1:T(8,128)(2,1)} async-done(((bf16[768,96]{0,1:T(8,128)(2,1)}), bf16[768,768]{0,1:T(8,128)(2,1)}) %all-gather.15.cloned.1.call-update) | async-done | bytes 1179664 | tf_op jit(solution)/shard_map/all_gather | solution.py:212
  324.9 28.3 %all-gather.13.cloned.1.call-done = bf16[2048,768]{1,0:T(8,128)(2,1)} async-done(((bf16[512,768]{1,0:T(8,128)(2,1)}), bf16[2048,768]{1,0:T(8,128)(2,1)}) %all-gather.13.cloned.1.call-update) | async-done | bytes 3145744 | tf_op jit(solution)/shard_map/all_gather | solution.py:217
  353.3 11.1 %convert_reduce_fusion = (f32[768]{0:T(1024)}, bf16[2048,768]{1,0:T(8,128)(2,1)S(1)}) fusion(f32[2048,768]{1,0:T(8,128)} %get-tuple-element.413, f32[2048,768]{1,0:T(8,128)} %get-tuple-element.428, f32[768]{0:T(1024)S(1)} %copy-done.41, bf16[2048,768]{1,0:T(8,128)(2,1)} %all-gather.13.cloned.1.call-done, bf16[768,768]{0,1:T(8,128)(2,1)} %all-gather.15.cloned.1.call-done), kind=kOutput, calls=%fused_computation.66 | convolution fusion | flops 2442657024 | bytes 20060160 | tf_op jit(solution)/shard_map/dot_general | solution.py:51
  370.2 38.0 %reduce-scatter.15.cloned.1.call-done = bf16[512,768]{1,0:T(8,128)(2,1)} async-done(((bf16[2048,768]{1,0:T(8,128)(2,1)}), bf16[512,768]{1,0:T(8,128)(2,1)}) %reduce-scatter.15.cloned.1.call-update) | async-done | bytes 786448 | tf_op jit(solution)/shard_map/reduce_scatter | solution.py:223
  416.9 28.4 %all-gather.17.cloned.1.call-done = bf16[2048,768]{1,0:T(8,128)(2,1)} async-done(((bf16[512,768]{1,0:T(8,128)(2,1)}), bf16[2048,768]{1,0:T(8,128)(2,1)}) %all-gather.17.cloned.1.call-update) | async-done | bytes 3145744 | tf_op jit(solution)/shard_map/all_gather | solution.py:229
  450.1 57.5 %while.56 = (s32[]{:T(128)}, bf16[2,1024,3,64]{3,2,1,0:T(4,128)(2,1)}, bf16[2,1024,3,64]{1,3,2,0:T(8,128)(2,1)}, bf16[2,1024,3,64]{1,3,2,0:T(8,128)(2,1)}, bf16[...) while((s32[]{:T(128)}, ...), condition=%wide.region_21.22_spmd, body=%wide.region_17.21_spmd.sunk | while | flops 1031798272 | bytes 74459688 | solution.py:232
  455.9 18.2 %while.58 = (s32[]{:T(128)}, f32[1024,3,64]{0,2,1:T(8,128)S(1)}, f32[1024,3,64]{0,2,1:T(8,128)}, bf16[2,512,3,64]{1,3,2,0:T(8,128)(2,1)S(1)}, bf16[2,512,3,64]{1...) while((s32[]{:T(128)}, f32[1024,3,64]{0,2,1:T(8,128)S(1)}, ...), condition=%wide.region_20.20_spmd.clone, body=%wide.region_18.19_spmd.clone.sunk | while | flops 1031405056 | bytes 58837208 | solution.py:118
  484.6 18.2 %while.58 = (s32[]{:T(128)}, f32[1024,3,64]{0,2,1:T(8,128)S(1)}, f32[1024,3,64]{0,2,1:T(8,128)}, bf16[2,512,3,64]{1,3,2,0:T(8,128)(2,1)S(1)}, bf16[2,512,3,64]{1...) while((s32[]{:T(128)}, f32[1024,3,64]{0,2,1:T(8,128)S(1)}, ...), condition=%wide.region_20.20_spmd.clone, body=%wide.region_18.19_spmd.clone.sunk | while | flops 1031405056 | bytes 58837208 | solution.py:118
  534.4 7.0 fusion.72
  541.7 7.0 fusion.73
  560.4 40.9 %all-reduce = (f32[768]{0:T(1024)}, f32[768]{0:T(1024)}, f32[768]{0:T(1024)}, f32[768]{0:T(1024)}, f32[768]{0:T(1024)}, /*index=5*/f32[3072]{0:T(1024)}, f32[768]{0:T(1024)}, f32[768]{0:T(1024)}, f32[768]{0:T(1024)}) all-reduce(f32[768]{0:T(1024)S(1)} %dynamic_update_slice.38, ...), channel_id=1, replica_groups=mesh['dp'=8,'tensor'=4] {'dp','tensor'}, use_global_device_ids=true, to_apply=%region_25.26 | all-reduce | flops 9216 | bytes 73728 | tf_op jit(solution)/shard_map/psum | solution.py:268
  602.9 12.4 %reduce-scatter.17.cloned.1.call-done = bf16[512,768]{1,0:T(8,128)(2,1)} async-done(((bf16[2048,768]{1,0:T(8,128)(2,1)}), bf16[512,768]{1,0:T(8,128)(2,1)}) %reduce-scatter.17.cloned.1.call-update) | async-done | bytes 786448 | tf_op jit(solution)/shard_map/reduce_scatter | solution.py:255
  617.8 71.2 %reduce-scatter.21.cloned.1.call-done = f32[96,768]{1,0:T(8,128)} async-done(((f32[768,768]{1,0:T(8,128)}), f32[96,768]{1,0:T(8,128)}) %reduce-scatter.21.cloned.1.call-update) | async-done | bytes 294928 | tf_op jit(solution)/shard_map/reduce_scatter | solution.py:265
  689.0 73.2 %reduce-scatter.23.cloned.1.call-done = f32[768,96]{0,1:T(8,128)} async-done(((f32[768,768]{0,1:T(8,128)}), f32[768,96]{0,1:T(8,128)}) %reduce-scatter.23.cloned.1.call-update) | async-done | bytes 294928 | tf_op jit(solution)/shard_map/reduce_scatter | solution.py:266
  762.2 73.1 %reduce-scatter.19.cloned.1.call-done = f32[96,3,192]{2,0,1:T(8,128)} async-done(((f32[768,3,192]{2,0,1:T(8,128)}), f32[96,3,192]{2,0,1:T(8,128)}) %reduce-scatter.19.cloned.1.call-update) | async-done | bytes 221200 | tf_op jit(solution)/shard_map/reduce_scatter | solution.py:263
  (328 shorter events, 214.0 us)
Async XLA Ops:
  8.0 72.4 %all-gather.7.cloned.1.call-start = ((), (), s32[]{:S(2)}) async-start(), calls=%async_computation.8 | async-start | bytes 3932160 | tf_op jit(solution)/shard_map/all_gather | solution.py:169
  8.7 156.6 %reduce-scatter.11.cloned.1.call-start = ((), (), s32[]{:S(2)}) async-start(), calls=%async_computation.9 | async-start | bytes 3932160 | tf_op jit(solution)/shard_map/reduce_scatter | solution.py:182
  126.5 90.2 %all-gather.11.cloned.1.call-start = ((), (), s32[]{:S(2)}) async-start(), calls=%async_computation.11 | async-start | bytes 1327104 | tf_op jit(solution)/shard_map/all_gather | solution.py:162
  127.1 42.9 %copy-start.16 = (bf16[768,96]{0,1:T(8,128)(2,1)S(1)}, bf16[768,96]{0,1:T(8,128)(2,1)}, u32[]{:S(2)}) copy-start(bf16[768,96]{0,1:T(8,128)(2,1)} %param.36) | copy-start | bytes 442372
  127.1 89.6 %all-gather.9.cloned.1.call-start = ((), (), s32[]{:S(2)}) async-start(), calls=%async_computation.10 | async-start | bytes 3932160 | tf_op jit(solution)/shard_map/all_gather | solution.py:191
  168.5 45.2 %copy-start.25 = (f32[512]{0:T(512)}, f32[512]{0:T(512)S(1)}, u32[]{:S(2)}) copy-start(f32[512]{0:T(512)S(1)} %fusion.63) | copy-start | bytes 6148
  169.9 111.4 %reduce-scatter.13.cloned.1.call-start = ((), (), s32[]{:S(2)}) async-start(), calls=%async_computation.12 | async-start | bytes 3932160 | tf_op jit(solution)/shard_map/reduce_scatter | solution.py:195
  170.0 7.2 collective-permute-start
  177.2 7.8 collective-permute-start.1
  185.9 27.1 %collective-permute-start.2 = (bf16[768,384]{0,1:T(8,128)(2,1)}, bf16[768,384]{0,1:T(8,128)(2,1)S(1)}, u32[]{:S(2)}, u32[]{:S(2)}) collective-permute-start(bf16[768,384]{0,1:T(8,128)(2,1)} %pad_maximum_fusion), channel_id=1, source_target_pairs={{0,16},{4,20},{8,24},{12,28},{16,0},{20,4},{24,8},{28,12},{1,17},{... | collective-permute-start | bytes 1769480 | tf_op jit(solution)/shard_map/ppermute | solution.py:24
  187.3 48.1 %copy-start.40 = (f32[768]{0:T(1024)}, f32[768]{0:T(1024)S(1)}, u32[]{:S(2)}) copy-start(f32[768]{0:T(1024)S(1)} %dynamic_slice.62) | copy-start | bytes 9220
  242.5 82.4 %all-gather.15.cloned.1.call-start = ((), (), s32[]{:S(2)}) async-start(), calls=%async_computation.14 | async-start | bytes 1327104 | tf_op jit(solution)/shard_map/all_gather | solution.py:212
  243.2 110.0 %all-gather.13.cloned.1.call-start = ((), (), s32[]{:S(2)}) async-start(), calls=%async_computation.13 | async-start | bytes 3932160 | tf_op jit(solution)/shard_map/all_gather | solution.py:217
  287.6 65.7 %copy-start.41 = (f32[768]{0:T(1024)S(1)}, f32[768]{0:T(1024)}, u32[]{:S(2)}) copy-start(f32[768]{0:T(1024)} %copy-done.40) | copy-start | bytes 9220
  287.6 76.8 %copy-start.27 = (f32[512]{0:T(512)}, f32[512]{0:T(512)S(1)}, u32[]{:S(2)}) copy-start(f32[512]{0:T(512)S(1)} %negate_multiply_fusion.2) | copy-start | bytes 6148
  289.8 118.4 %reduce-scatter.15.cloned.1.call-start = ((), (), s32[]{:S(2)}) async-start(), calls=%async_computation.15 | async-start | bytes 3932160 | tf_op jit(solution)/shard_map/reduce_scatter | solution.py:223
  370.2 75.2 %all-gather.17.cloned.1.call-start = ((), (), s32[]{:S(2)}) async-start(), calls=%async_computation.16 | async-start | bytes 3932160 | tf_op jit(solution)/shard_map/all_gather | solution.py:229
  416.6 184.6 %reduce-scatter.25.cloned.1.call-start = ((), (), s32[]{:S(2)}) async-start(), calls=%async_computation.21 | async-start | bytes 884736
  512.2 103.1 %reduce-scatter.17.cloned.1.call-start = ((), (), s32[]{:S(2)}) async-start(), calls=%async_computation.17 | async-start | bytes 3932160 | tf_op jit(solution)/shard_map/reduce_scatter | solution.py:255
  534.3 154.6 %reduce-scatter.21.cloned.1.call-start = ((), (), s32[]{:S(2)}) async-start(), calls=%async_computation.19 | async-start | bytes 2654208 | tf_op jit(solution)/shard_map/reduce_scatter | solution.py:265
  541.4 220.7 %reduce-scatter.23.cloned.1.call-start = ((), (), s32[]{:S(2)}) async-start(), calls=%async_computation.20 | async-start | bytes 2654208 | tf_op jit(solution)/shard_map/reduce_scatter | solution.py:266
  548.7 286.5 %reduce-scatter.19.cloned.1.call-start = ((), (), s32[]{:S(2)}) async-start(), calls=%async_computation.18 | async-start | bytes 2654208 | tf_op jit(solution)/shard_map/reduce_scatter | solution.py:263
  555.5 59.8 %copy-start.10 = (f32[512,768]{1,0:T(8,128)S(1)}, f32[512,768]{1,0:T(8,128)}, u32[]{:S(2)}) copy-start(f32[512,768]{1,0:T(8,128)} %copy-done.9) | copy-start | bytes 4718596
  555.5 59.8 %copy-start.29 = (f32[512]{0:T(512)S(1)}, f32[512]{0:T(512)}, u32[]{:S(2)}) copy-start(f32[512]{0:T(512)} %copy-done.28) | copy-start | bytes 6148
  (47 other events, 560.9 us)
Sparse Core Ops, SparseCore 0:
  10.4 31.2 all-gather.6
  126.7 38.6 reduce-scatter.10
  370.3 37.8 reduce-scatter.14
  416.8 28.5 all-gather.16
Sparse Core Ops, SparseCore 1:
  129.2 42.2 all-gather.10
  173.4 26.7 all-gather.8
  242.6 38.6 reduce-scatter.12
  283.5 41.4 all-gather.14
  326.5 26.7 all-gather.12
  512.3 63.2 reduce-scatter.24
  578.0 37.3 reduce-scatter.16
  619.2 69.7 reduce-scatter.20
  692.9 69.2 reduce-scatter.22
  766.3 69.0 reduce-scatter.18
